TPU v7x, 768 devices: a whole 4x8x12 slice. The times are simulated.
768 devices in a mesh: dp: 32 (over y, z_lo), tensor: 24 (over z_hi, x, core).
Axes of the slice: x: 4, y: 8, z: 12 (z_hi: 3, z_lo: 4; z = z_hi * 4 + z_lo), core: 2. Of those that a mesh axis runs over, the one named last changes fastest.
Arguments:
- activations: bfloat16 [16384, 6144], P('dp', 'tensor'), may hold values from -6 to 6
- cotangent: bfloat16 [16384, 5120], P('dp'), may hold values from -0.046875 to 0.046875
- master: float32 [5120, 6144], P('dp', 'tensor'), may hold values from -0.078125 to 0.078125
- moment_one: float32 [5120, 6144], P('dp', 'tensor'), may hold values from -0.3 to 0.3
- moment_two: float32 [5120, 6144], P('dp', 'tensor'), may hold values from 0.0002 to 0.002
- prompts: bfloat16 [6144, 6144], P('dp', 'tensor'), may hold values from -6 to 6
Outputs:
- new_master: float32 [5120, 6144], P('dp', 'tensor')
- new_moment_one: float32 [5120, 6144], P('dp', 'tensor')
- new_moment_two: float32 [5120, 6144], P('dp', 'tensor')
- projected: bfloat16 [6144, 5120], P(('dp', 'tensor'))
All inputs are finite; a program needn't handle non-finite values.
Results may differ from a plain program's by a relative error of at most 0.03.
Values may be sent and summed in bfloat16 or wider, within the bound.
A program may use at most 32 MiB of HBM per device.

v0:
```python
import jax
import jax.numpy as jnp
from jax import lax
from jax.sharding import Mesh
from jax.sharding import PartitionSpec as P

DP = ("dp_0", "dp_1")
DP_TENSOR = ("dp_0", "dp_1", "tensor")


def own_rows(terms, axes):
    total = terms.astype(jnp.bfloat16)
    for axis in axes:
        total = lax.psum_scatter(total, axis, scatter_dimension=0, tiled=True)
    return total.astype(jnp.float32)


def sent_to_all(value, axis):
    copies = jnp.broadcast_to(value, (lax.axis_size(axis), *value.shape))
    return lax.all_to_all(copies, axis, split_axis=0, concat_axis=0, tiled=True)


def laid_out(pieces, dim):
    shape = list(pieces.shape[1:])
    shape[dim] *= pieces.shape[0]
    return jnp.moveaxis(pieces, 0, dim).reshape(shape)


def gather_directly(value, axis, dim):
    pieces = sent_to_all(value, axis)
    return laid_out(pieces, dim)


def local(activations, cotangent, master, moment_one, moment_two, prompts):
    grad = own_rows(
        lax.dot_general(
            cotangent, activations, (((0,), (0,)), ((), ())), preferred_element_type=jnp.float32
        ),
        DP,
    )
    new_one = 0.9 * moment_one + 0.1 * grad
    new_two = 0.999 * moment_two + 0.001 * grad * grad
    first = new_one / (1.0 - 0.9**50)
    second = new_two / (1.0 - 0.999**50)
    new_master = master - 0.003 * (first / (jnp.sqrt(second) + 1e-08) + 0.01 * master)
    rollout_weight = new_master.astype(jnp.bfloat16)
    partial_out = lax.dot_general(
        prompts,
        gather_directly(rollout_weight, DP, 0),
        (((1,), (1,)), ((), ())),
        preferred_element_type=jnp.float32,
    )
    projected = lax.psum_scatter(
        partial_out.astype(jnp.bfloat16), "tensor", scatter_dimension=0, tiled=True
    )
    return (new_master, new_one, new_two, projected)


def solution(mesh):
    torus = Mesh(mesh.devices.reshape(8, 4, mesh.shape["tensor"]), ("dp_0", "dp_1", "tensor"))
    in_specs = (
        P(DP, "tensor"),
        P(DP, None),
        P(DP, "tensor"),
        P(DP, "tensor"),
        P(DP, "tensor"),
        P(DP, "tensor"),
    )
    out_specs = (P(DP, "tensor"), P(DP, "tensor"), P(DP, "tensor"), P(DP_TENSOR, None))
    return jax.shard_map(local, mesh=torus, in_specs=in_specs, out_specs=out_specs, check_vma=False)
```

profile of v0, /device:TPU:1, one launch (start us, length us, event | category | flops | bytes accessed | tf_op | source)
XLA Modules:
  0.0 314.5 jit_solution(17937036849344679179)
XLA Ops:
  7.2 0.0 copy-start
  7.2 0.0 reduce-scatter.4.cloned.1.call-start
  7.2 0.9 copy-done
  8.1 5.6 %convolution_convert_fusion = bf16[5120,256]{1,0:T(8,128)(2,1)} fusion(bf16[512,5120]{1,0:T(8,128)(2,1)} %param.7, bf16[512,256]{1,0:T(8,128)(2,1)S(1)} %copy-done), kind=kOutput, calls=%fused_computation | convolution fusion | flops 1343488000 | bytes 8126464 | tf_op jit(solution)/shard_map/dot_general | solution.py:36
  13.7 0.0 copy-start.1
  13.7 0.0 copy-start.2
  13.7 0.0 copy-start.3
  13.7 0.0 reduce-scatter.4.cloned.1.call-update
  13.7 0.0 reduce-scatter.6.cloned.1.call-start
  13.8 53.2 %reduce-scatter.4.cloned.1.call-done = bf16[640,256]{1,0:T(8,128)(2,1)} async-done(((bf16[5120,256]{1,0:T(8,128)(2,1)}), bf16[640,256]{1,0:T(8,128)(2,1)}) %reduce-scatter.4.cloned.1.call-update) | async-done | bytes 327696 | tf_op jit(solution)/shard_map/reduce_scatter | solution.py:14
  67.0 0.0 reduce-scatter.6.cloned.1.call-update
  67.0 0.0 reduce-scatter.8.cloned.1.call-start
  67.1 36.2 %reduce-scatter.6.cloned.1.call-done = bf16[160,256]{1,0:T(8,128)(2,1)} async-done(((bf16[640,256]{1,0:T(8,128)(2,1)}), bf16[160,256]{1,0:T(8,128)(2,1)}) %reduce-scatter.6.cloned.1.call-update) | async-done | bytes 81936 | tf_op jit(solution)/shard_map/reduce_scatter | solution.py:14
  103.3 0.0 copy-done.1
  103.3 0.0 copy-done.2
  103.3 0.0 copy-done.3
  103.3 1.7 fusion.3
  105.0 0.3 broadcast_in_dim.3
  105.3 0.0 copy-start.4
  105.3 66.9 %all_to_all.5 = bf16[32,160,256]{2,1,0:T(8,128)(2,1)S(1)} all-to-all(bf16[32,160,256]{2,1,0:T(8,128)(2,1)S(1)} %broadcast_in_dim.3), channel_id=1, replica_groups=mesh['dp_0'=8,'dp_1'=4,'tensor'=24] {'dp_0','dp_1'}, dimensions={0} | all-to-all | bytes 5242880 | tf_op jit(solution)/shard_map/all_to_all | solution.py:20
  172.3 0.0 copy-done.4
  172.3 2.3 fusion
  174.6 0.0 reduce-scatter.8.cloned.1.call-update
  174.6 133.3 %reduce-scatter.8.cloned.1.call-done = bf16[8,5120]{1,0:T(8,128)(2,1)} async-done(((bf16[192,5120]{1,0:T(8,128)(2,1)}), bf16[8,5120]{1,0:T(8,128)(2,1)}) %reduce-scatter.8.cloned.1.call-update) | async-done | bytes 81936 | tf_op jit(solution)/shard_map/reduce_scatter | solution.py:53
Async XLA Ops:
  7.2 1.0 copy-start
  7.2 59.8 %reduce-scatter.4.cloned.1.call-start = ((), (), s32[]{:S(2)}) async-start(), calls=%async_computation.4 | async-start | bytes 2949120 | tf_op jit(solution)/shard_map/reduce_scatter | solution.py:14
  13.7 89.6 %copy-start.1 = (f32[160,256]{1,0:T(8,128)S(1)}, f32[160,256]{1,0:T(8,128)}, u32[]{:S(2)}) copy-start(f32[160,256]{1,0:T(8,128)} %param.8) | copy-start | bytes 491524
  13.7 89.6 %copy-start.2 = (f32[160,256]{1,0:T(8,128)S(1)}, f32[160,256]{1,0:T(8,128)}, u32[]{:S(2)}) copy-start(f32[160,256]{1,0:T(8,128)} %param.9) | copy-start | bytes 491524
  13.7 89.6 %copy-start.3 = (f32[160,256]{1,0:T(8,128)S(1)}, f32[160,256]{1,0:T(8,128)}, u32[]{:S(2)}) copy-start(f32[160,256]{1,0:T(8,128)} %param.10) | copy-start | bytes 491524
  13.7 89.5 %reduce-scatter.6.cloned.1.call-start = ((), (), s32[]{:S(2)}) async-start(), calls=%async_computation.5 | async-start | bytes 409600 | tf_op jit(solution)/shard_map/reduce_scatter | solution.py:14
  67.0 240.9 %reduce-scatter.8.cloned.1.call-start = ((), (), s32[]{:S(2)}) async-start(), calls=%async_computation.6 | async-start | bytes 2048000 | tf_op jit(solution)/shard_map/reduce_scatter | solution.py:53
  105.3 67.0 %copy-start.4 = (bf16[192,256]{1,0:T(8,128)(2,1)S(1)}, bf16[192,256]{1,0:T(8,128)(2,1)}, u32[]{:S(2)}) copy-start(bf16[192,256]{1,0:T(8,128)(2,1)} %param.11) | copy-start | bytes 294916
Sparse Core Ops, SparseCore 0:
  13.9 53.0 reduce-scatter.3
  70.1 33.1 reduce-scatter.5
  174.8 133.1 reduce-scatter.7
where the time goes:
time: 315 us; the launch traced here: 314 us
  waiting for transfers between devices  223 us (71%)
  blocking collectives  66.9 us (21%)
  between operations  13.8 us (4%)
  matrix products  7.93 us (3%)
    reduce_scatter x1, waiting for transfers between devices, local(): lax.psum_scatter(partial_out.astype(jnp.bfloat16), 'tensor', scatter_dime...  133 us
    reduce_scatter x2, waiting for transfers between devices, own_rows(): total = lax.psum_scatter(total, axis, scatter_dimension=0, tiled=True)  89.4 us
    all_to_all x1, blocking collectives, sent_to_all(): return lax.all_to_all(copies, axis, split_axis=0, concat_axis=0, tiled=True)  66.9 us
  transfers between devices with their start and end apart: 3, of which 3 were waited for; matrix products, arithmetic and copies ran while one was open for 0% of the time, Pallas kernels for 0%

commit v1 on v0

v1 whole, which is shorter than its diff:
```python
import functools

import jax
import jax.numpy as jnp
from jax import lax
from jax.experimental import pallas as pl
from jax.experimental.pallas import tpu as pltpu
from jax.sharding import Mesh
from jax.sharding import PartitionSpec as P

AXES = ("y", "zl", "zh", "x", "c")
NY, NL, NH, NX, NC = 8, 4, 3, 4, 2
NZ = NL * NH
BF = jnp.bfloat16
F32 = jnp.float32

ROWS = 160
COLS = 256
OUTS = NY * ROWS // 2
SUB = NH * 16


def kernel(
    act_hbm, cot_hbm, master_hbm, one_hbm, two_hbm, prompts_hbm,
    master_out, one_out, two_out, proj_out,
    act, cot, state, new_state, own_prompts, prompts, terms, ring, ring_z, weight,
    own_part, core_out, core_in, x_out, x_in, z_out, z_in, half_sum, half_in, proj,
    load_sem, cot_sem, store_sem, p_send, p_recv, y_send, y_recv, z_send, z_recv,
    w_send, w_recv, c_send, c_recv, x_send, x_recv, f_send, f_recv, h_send, h_recv,
):
    y, zl, zh, x, c = (lax.axis_index(axis) for axis in AXES)
    sent = []

    def go(src, dst, send_sem, recv_sem, to):
        copy = pltpu.make_async_remote_copy(
            src_ref=src, dst_ref=dst, send_sem=send_sem, recv_sem=recv_sem,
            device_id=to, device_id_type=pl.DeviceIdType.MESH,
        )
        copy.start()
        return copy

    def send(src, dst, send_sem, recv_sem, to):
        sent.append(go(src, dst, send_sem, recv_sem, to))

    def arrived(dst, recv_sem):
        pltpu.make_async_copy(dst, dst, recv_sem).wait()

    def cot_copy(r):
        first = pl.multiple_of(lax.rem(y + r, NY) * 640, 640)
        return pltpu.make_async_copy(cot_hbm.at[:, pl.ds(first, 640)], cot.at[r], cot_sem.at[r])

    act_copy = pltpu.make_async_copy(act_hbm, act, load_sem.at[0])
    act_copy.start()
    order = (4, 3, 5, 2, 6, 1, 7, 0)
    for r in order[:3]:
        cot_copy(r).start()
    prompt_copies = [
        pltpu.make_async_copy(prompts_hbm.at[:, i], own_prompts.at[i], load_sem.at[1 + i]) for i in range(NX)
    ]
    for copy in prompt_copies:
        copy.start()
    for r in order[3:]:
        cot_copy(r).start()
    state_copies = [
        pltpu.make_async_copy(ref, state.at[i], load_sem.at[5 + i])
        for i, ref in enumerate((master_hbm, one_hbm, two_hbm))
    ]
    for copy in state_copies:
        copy.start()

    barrier = pltpu.get_barrier_semaphore()
    peers = [{"y": lax.rem(y + 1, NY)}, {"y": lax.rem(y + NY - 1, NY)}]
    peers += [{"x": lax.rem(x + 1, NX)}, {"x": lax.rem(x + NX - 1, NX)}, {"c": 1 - c}]
    for dh in range(NH):
        for dl in range(NL):
            if dh or dl:
                peers.append({"zh": lax.rem(zh + dh, NH), "zl": lax.rem(zl + dl, NL)})
    for peer in peers:
        pl.semaphore_signal(barrier, inc=1, device_id=peer, device_id_type=pl.DeviceIdType.MESH)

    def term(r):
        cot_copy(r).wait()
        for b in range(5):
            block = lax.dot_general(
                cot[r, :, b * 128 : (b + 1) * 128], act[...],
                (((0,), (0,)), ((), ())), preferred_element_type=F32,
            )
            terms[r, b * 128 : (b + 1) * 128, :] = block.astype(BF)

    act_copy.wait()
    term(4)
    for copy in prompt_copies:
        copy.wait()
    pl.semaphore_wait(barrier, len(peers))

    step = (1, NY - 1)

    def z_rel(i):
        return lax.rem(zl + 1 + i, NL)

    def rows_of(i):
        return pl.ds(pl.multiple_of(z_rel(i) * ROWS, ROWS), ROWS)

    for k in (4, 3, 2, 1):
        if k < 4:
            term(k)
            term(NY - k)
        for i in range(NL):
            rows = rows_of(i)
            for d in range(2):
                r = (step[d] * k) % NY
                half = slice(d * 128, (d + 1) * 128)
                cols = half if k == 4 else slice(0, COLS)
                if k < 4:
                    got = half if k == 3 else slice(0, COLS)
                    arrived(ring.at[d, k, i, :, got], y_recv.at[d, k, i])
                    total = terms[r, rows, got].astype(F32) + ring[d, k, i, :, got].astype(F32)
                    terms[r, rows, got] = total.astype(BF)
                send(
                    terms.at[r, rows, cols], ring.at[d, k - 1, i, :, cols],
                    y_send.at[d, k, i], y_recv.at[d, k - 1, i], {"y": lax.rem(y + step[d], NY)},
                )
        if k == 4:
            for dl in range(1, NL):
                send(
                    own_prompts, prompts.at[zl], p_send.at[dl - 1], p_recv.at[dl - 1],
                    {"zl": lax.rem(zl + dl, NL)},
                )
            prompts[zl] = own_prompts[...]
    term(0)

    for i in range(NL):
        rows = rows_of(i)
        for d in range(2):
            arrived(ring.at[d, 0, i], y_recv.at[d, 0, i])
        total = terms[0, rows, :].astype(F32) + ring[0, 0, i].astype(F32) + ring[1, 0, i].astype(F32)
        if i < NL - 1:
            terms[0, rows, :] = total.astype(BF)
            send(
                terms.at[0, rows, :], ring_z.at[i], z_send.at[i], z_recv.at[i],
                {"zl": lax.rem(zl + 1 + i, NL)},
            )
    grad = total
    for copy in state_copies:
        copy.wait()
    for i in range(NL - 1):
        arrived(ring_z.at[i], z_recv.at[i])
        grad = grad + ring_z[i].astype(F32)

    new_one = 0.9 * state[1] + 0.1 * grad
    new_two = 0.999 * state[2] + 0.001 * grad * grad
    first = new_one / (1.0 - 0.9**50)
    second = new_two / (1.0 - 0.999**50)
    old = state[0]
    new_master = old - 0.003 * (first / (jnp.sqrt(second) + 1e-08) + 0.01 * old)
    weight[y] = new_master.astype(BF)
    new_state[0] = new_master
    new_state[1] = new_one
    new_state[2] = new_two

    def piece(n):
        return pl.ds((n // 2) * 80, 80), pl.ds((n % 2) * 128, 128)

    for s in range(1, 5):
        for n in range(4):
            for d in range(2):
                if s == 4 and n // 2 != d:
                    continue
                origin = lax.rem(y + (NY - step[d]) * (s - 1), NY)
                part = weight.at[(origin, *piece(n))]
                if s > 1:
                    arrived(part, w_recv.at[d, s - 2, n])
                send(
                    part, part, w_send.at[d, s - 1, n], w_recv.at[d, s - 1, n],
                    {"y": lax.rem(y + step[d], NY)},
                )
        if s == 1:
            stores = [
                pltpu.make_async_copy(new_state.at[i], ref, store_sem.at[i])
                for i, ref in enumerate((master_out, one_out, two_out))
            ]
            for copy in stores:
                copy.start()
            for dl in range(1, NL):
                arrived(prompts.at[0], p_recv.at[dl - 1])
    for s in (3, 4):
        for n in range(4):
            for d in range(2):
                if s == 4 and n // 2 != d:
                    continue
                if s == 3 and n // 2 == d:
                    continue
                origin = lax.rem(y + (NY - step[d]) * s, NY)
                arrived(weight.at[(origin, *piece(n))], w_recv.at[d, s - 1, n])

    x_order = (2, 1, 3, 0)

    def project(i, core):
        x_to = lax.rem(x + x_order[i], NX)
        lhs = jnp.concatenate([prompts[n, x_to].reshape(SUB, COLS) for n in range(NL)], axis=0)
        rhs = weight[pl.ds(4 * core, 4)].reshape(OUTS, COLS)
        return lax.dot_general(lhs, rhs, (((1,), (1,)), ((), ())), preferred_element_type=F32)

    for i in range(NX):
        core_out[i] = project(i, 1 - c).astype(BF)
        send(core_out.at[i], core_in.at[i], c_send.at[i], c_recv.at[i], {"c": 1 - c})
        own_part[i] = project(i, c)

    x_dir = (1, NX - 1)

    def part_sum(i, n):
        rows = slice(n * SUB, (n + 1) * SUB)
        return own_part[i, rows, :] + core_in[i, rows, :].astype(F32)

    def x_send_to(d, i, n, k):
        send(
            x_out.at[i, n], x_in.at[d, k, n], x_send.at[d, k, n], x_recv.at[d, k, n],
            {"x": lax.rem(x + x_dir[d], NX)},
        )

    def far(d, n):
        x_out[0, n] = part_sum(0, n).astype(BF)
        x_send_to(d, 0, n, 1)

    def near(d, n):
        total = part_sum(1 + d, n)
        if n // 2 == d:
            arrived(x_in.at[d, 1, n], x_recv.at[d, 1, n])
            total = total + x_in[d, 1, n].astype(F32)
        x_out[1 + d, n] = total.astype(BF)
        x_send_to(d, 1 + d, n, 0)

    arrived(core_in.at[0], c_recv.at[0])
    far(0, 0)
    far(1, 2)
    arrived(core_in.at[1], c_recv.at[1])
    near(0, 2)
    arrived(core_in.at[2], c_recv.at[2])
    near(1, 0)
    far(0, 1)
    far(1, 3)
    near(0, 0)
    near(1, 2)
    near(0, 3)
    near(1, 1)
    near(0, 1)
    near(1, 3)
    arrived(core_in.at[3], c_recv.at[3])

    me = zh * NL + zl
    for n in (0, 2, 1, 3):
        total = part_sum(3, n)
        for d in range(2):
            arrived(x_in.at[d, 0, n], x_recv.at[d, 0, n])
            total = total + x_in[d, 0, n].astype(F32)
        z_out[n] = total.astype(BF).reshape(NH, 16, OUTS)
        for h in range(NH):
            to = h * NL + n

            @pl.when(me != to)
            def _():
                go(z_out.at[n, h], z_in.at[me], f_send.at[to], f_recv.at[me], {"zh": h, "zl": n})

    z_in[me] = z_out[zl, zh]
    for at in range(NZ):

        @pl.when(me != at)
        def _():
            arrived(z_in.at[at], f_recv.at[at])

    for n in range(NL):
        half_sum[n] = z_in[n].astype(F32) + z_in[NL + n].astype(F32) + z_in[2 * NL + n].astype(F32)
    theirs = pl.ds(pl.multiple_of(8 * (1 - c), 8), 8)
    mine = pl.ds(pl.multiple_of(8 * c, 8), 8)
    send(half_sum.at[:, theirs, :], half_in, h_send.at[0], h_recv.at[0], {"c": 1 - c})

    def laid_out(read):
        parts = [read(n) for n in range(NL)]
        return jnp.concatenate(
            [parts[n][:, j * ROWS : (j + 1) * ROWS] for j in range(4) for n in range(NL)], axis=1
        ).astype(BF)

    own_at = pl.ds(pl.multiple_of(c * 2560, 2560), 2560)
    proj[:, own_at] = laid_out(lambda n: half_sum[n, mine, :])
    arrived(half_in, h_recv.at[0])
    other_at = pl.ds(pl.multiple_of((1 - c) * 2560, 2560), 2560)
    proj[:, other_at] = laid_out(lambda n: half_in[n])
    last = pltpu.make_async_copy(proj, proj_out, store_sem.at[3])
    last.start()

    for copy in sent:
        copy.wait_send()
    for to in range(NZ):

        @pl.when(me != to)
        def _():
            pltpu.make_async_copy(z_in.at[0], z_in.at[0], f_send.at[to]).wait()

    for copy in stores:
        copy.wait()
    last.wait()


def local(activations, cotangent, master, moment_one, moment_two, prompts):
    any_space = pl.BlockSpec(memory_space=pl.ANY)
    dma = pltpu.SemaphoreType.DMA
    weight_shape = jax.ShapeDtypeStruct((ROWS, COLS), F32)
    return pl.pallas_call(
        kernel,
        out_shape=(weight_shape, weight_shape, weight_shape, jax.ShapeDtypeStruct((8, 5120), BF)),
        in_specs=[any_space] * 6,
        out_specs=[any_space] * 4,
        scratch_shapes=[
            pltpu.VMEM((512, COLS), BF),
            pltpu.VMEM((NY, 512, 640), BF),
            pltpu.VMEM((3, ROWS, COLS), F32),
            pltpu.VMEM((3, ROWS, COLS), F32),
            pltpu.VMEM((NX, NH, 16, COLS), BF),
            pltpu.VMEM((NL, NX, NH, 16, COLS), BF),
            pltpu.VMEM((NY, 640, COLS), BF),
            pltpu.VMEM((2, 4, NL, ROWS, COLS), BF),
            pltpu.VMEM((NL - 1, ROWS, COLS), BF),
            pltpu.VMEM((NY, ROWS, COLS), BF),
            pltpu.VMEM((NX, NL * SUB, OUTS), F32),
            pltpu.VMEM((NX, NL * SUB, OUTS), BF),
            pltpu.VMEM((NX, NL * SUB, OUTS), BF),
            pltpu.VMEM((3, NL, SUB, OUTS), BF),
            pltpu.VMEM((2, 2, NL, SUB, OUTS), BF),
            pltpu.VMEM((NL, NH, 16, OUTS), BF),
            pltpu.VMEM((NZ, 16, OUTS), BF),
            pltpu.VMEM((NL, 16, OUTS), F32),
            pltpu.VMEM((NL, 8, OUTS), F32),
            pltpu.VMEM((8, 5120), BF),
            dma((8,)), dma((NY,)), dma((4,)),
            dma((3,)), dma((3,)),
            dma((2, 5, NL)), dma((2, 4, NL)),
            dma((3,)), dma((3,)),
            dma((2, 4, 4)), dma((2, 4, 4)),
            dma((NX,)), dma((NX,)),
            dma((2, 2, NL)), dma((2, 2, NL)),
            dma((NZ,)), dma((NZ,)),
            dma((1,)), dma((1,)),
        ],
        compiler_params=pltpu.CompilerParams(collective_id=0, has_side_effects=True),
        name="step",
    )(activations, cotangent, master, moment_one, moment_two, prompts.reshape(NH, NX, 16, COLS))


def solution(mesh):
    torus = Mesh(mesh.devices.reshape(NY, NL, NH, NX, NC), AXES)
    dp, tensor = ("y", "zl"), ("zh", "x", "c")
    both = P(dp, tensor)
    in_specs = (both, P(dp, None), both, both, both, both)
    out_specs = (both, both, both, P(dp + tensor, None))
    return jax.shard_map(local, mesh=torus, in_specs=in_specs, out_specs=out_specs, check_vma=False)
```

time: 315 us -> 93.7 us (0.30)
  waiting for transfers between devices: 223 us -> 0 us
  Pallas kernels: 0 us -> 86.5 us
  blocking collectives: 66.9 us -> 0 us
  between operations: 13.8 us -> 0.64 us
  matrix products: 7.93 us -> 0 us
  local copies, waits for them, and re-layouts: 1.2 us -> 6.3 us
    reduce_scatter x3 -> x0, waiting for transfers between devices: 223 us -> none  [the longest x1 133 us: local(): lax.psum_scatter(partial_out.astype(jnp.bfloat16), 'tensor', scatter_dime...]
    pallas_call x0 -> x1, Pallas kernels: none -> 86.5 us  [local(): pl.pallas_call(kernel, out_shape=(weight_shape, weight_shape, weight_shap...]
    all_to_all x1 -> x0, blocking collectives: 66.9 us -> none  [sent_to_all(): return lax.all_to_all(copies, axis, split_axis=0, concat_axis=0, tiled=True)]
    dot_general x2 -> x0, matrix products: 7.93 us -> none  [the longest x1 5.59 us: local(): lax.dot_general(cotangent, activations, (((0,), (0,)), ((), ())), preferr...]
    unnamed x10 -> x4, local copies, waits for them, and re-layouts: 0.92 us -> 6.3 us
  transfers between devices with their start and end apart: 3 -> 0, of which waited for: 3 -> 0; matrix products, arithmetic and copies ran while one was open for 0% -> 0% of each run, Pallas kernels for 0% -> 0%
where the time goes in v1:
time: 93.7 us; the launch traced here: 93.5 us
  Pallas kernels  86.5 us (92%)
  local copies, waits for them, and re-layouts  6.3 us (7%)
    pallas_call x1, Pallas kernels, local(): pl.pallas_call(kernel, out_shape=(weight_shape, weight_shape, weight_shap...  86.5 us
    unnamed x4, local copies, waits for them, and re-layouts  6.3 us

profile of v1, /device:TPU:1, one launch (start us, length us, event | category | flops | bytes accessed | tf_op | source)
XLA Modules:
  0.0 93.5 jit_solution(16831990832321528799)
XLA Ops:
  0.6 86.5 %step.1 = (f32[160,256]{1,0:T(8,128)}, f32[160,256]{1,0:T(8,128)}, f32[160,256]{1,0:T(8,128)}, bf16[8,5120]{1,0:T(8,128)(2,1)}) custom-call(bf16[512,256]{1,0:T(8,128)(2,1)} %act_hbm.1, bf16[512,5120]{1,0:T(8,128)(2,1)} %cot_hbm.1, f32[160,256]{1,0:T(8,128)} %master_hbm.1, f32[160,256]{1,0:T(8,128)} %one_hbm.1, f32[160,256]{1,0:T(8,128)} %two_hbm.1, ...), custom_call_target="tpu_custom_call" | custom-call | tf_op jit(solution)/shard_map/step/pallas_call | solution.py:308
  87.2 1.6 %copy.14 = f32[160,256]{1,0:T(8,128)} copy(f32[160,256]{1,0:T(8,128)} %get-tuple-element.8) | data formatting | bytes 327680
  88.8 1.6 %copy.15 = f32[160,256]{1,0:T(8,128)} copy(f32[160,256]{1,0:T(8,128)} %get-tuple-element.9) | data formatting | bytes 327680
  90.4 1.6 %copy.16 = f32[160,256]{1,0:T(8,128)} copy(f32[160,256]{1,0:T(8,128)} %get-tuple-element.10) | data formatting | bytes 327680
  92.0 1.5 %copy.17 = bf16[8,5120]{1,0:T(8,128)(2,1)} copy(bf16[8,5120]{1,0:T(8,128)(2,1)} %get-tuple-element.11) | data formatting | bytes 163840

commit v2 on v1

v2 whole, which is shorter than its diff:
```python
import jax
import jax.numpy as jnp
from jax import lax
from jax.experimental import pallas as pl
from jax.experimental.pallas import tpu as pltpu
from jax.sharding import Mesh
from jax.sharding import PartitionSpec as P

AXES = ("y", "zl", "zh", "x", "c")
NY, NL, NH, NX, NC = 8, 4, 3, 4, 2
NZ = NL * NH
BF = jnp.bfloat16
F32 = jnp.float32

ROWS = 160
FIRST_Y = 112
REST = ROWS - FIRST_Y
COLS = 256
OUTS = 4 * ROWS
SUB = NH * 16
PLACE = (0, 1, 7, 2, 6, 3, 5, 4)
SLOT = tuple(PLACE.index(r) for r in range(NY))
MESH = pl.DeviceIdType.MESH


def kernel(
    act_hbm, cot_hbm, master_hbm, one_hbm, two_hbm, prompts_hbm,
    state_out, proj_out,
    act, cot, state, new_state, own_prompts, prompts, terms, ring, ring_z, rest_z, rest_y, rest_sum,
    weight, own_part, core_out, core_in, x_out, x_in, z_out, z_in, half_sum, half_in, proj,
    load_sem, cot_sem, store_sem, p_send, p_recv, y_send, y_recv, z_send, z_recv,
    rz_send, rz_recv, ry_send, ry_recv,
    w_send, w_recv, c_send, c_recv, x_send, x_recv, f_send, f_recv, h_send, h_recv,
):
    y, zl, zh, x, c = (lax.axis_index(axis) for axis in AXES)
    sent = []

    def go(src, dst, send_sem, recv_sem, to):
        copy = pltpu.make_async_remote_copy(
            src_ref=src, dst_ref=dst, send_sem=send_sem, recv_sem=recv_sem,
            device_id=to, device_id_type=MESH,
        )
        copy.start()
        return copy

    def send(src, dst, send_sem, recv_sem, to):
        sent.append(go(src, dst, send_sem, recv_sem, to))

    def arrived(dst, recv_sem):
        pltpu.make_async_copy(dst, dst, recv_sem).wait()

    def cot_copy(r):
        first = pl.multiple_of(lax.rem(y + r, NY) * 640, 640)
        return pltpu.make_async_copy(cot_hbm.at[:, pl.ds(first, 640)], cot.at[r], cot_sem.at[r])

    act_copy = pltpu.make_async_copy(act_hbm, act, load_sem.at[0])
    act_copy.start()
    for r in (4, 3, 5, 2, 6, 1, 7, 0):
        cot_copy(r).start()
    prompt_copies = [
        pltpu.make_async_copy(prompts_hbm.at[:, i], own_prompts.at[i], load_sem.at[1 + i]) for i in range(NX)
    ]
    state_copies = [
        pltpu.make_async_copy(ref, state.at[i], load_sem.at[5 + i])
        for i, ref in enumerate((master_hbm, one_hbm, two_hbm))
    ]
    for copy in prompt_copies + state_copies:
        copy.start()

    barrier = pltpu.get_barrier_semaphore()
    peers = [{"y": lax.rem(y + i, NY)} for i in range(1, NY)]
    peers += [{"zl": lax.rem(zl + i, NL)} for i in range(1, NL)]
    peers += [{"x": lax.rem(x + 1, NX)}, {"x": lax.rem(x + NX - 1, NX)}, {"c": 1 - c}]
    for peer in peers:
        pl.semaphore_signal(barrier, inc=1, device_id=peer, device_id_type=MESH)
    me = zh * NL + zl
    own_half = zl // 2 == c
    for h in range(NH):
        for n in range(NL):

            @pl.when(jnp.logical_or(me != h * NL + n, jnp.logical_not(own_half)))
            def _():
                pl.semaphore_signal(
                    barrier, inc=1, device_id={"zh": h, "zl": n, "c": zl // 2}, device_id_type=MESH
                )

    def term(r):
        cot_copy(r).wait()
        for b in range(5):
            block = lax.dot_general(
                cot[r, :, b * 128 : (b + 1) * 128], act[...],
                (((0,), (0,)), ((), ())), preferred_element_type=F32,
            )
            terms[r, b * 128 : (b + 1) * 128, :] = block.astype(BF)

    def z_rel(i):
        return lax.rem(zl + 1 + i, NL)

    def rows_of(i):
        return pl.ds(pl.multiple_of(z_rel(i) * ROWS, ROWS), FIRST_Y)

    def rest_of(i):
        return pl.ds(pl.multiple_of(z_rel(i) * ROWS + FIRST_Y, 16), REST)

    def rest_over_z(r):
        for i in range(NL - 1):
            send(
                terms.at[r, rest_of(i), :], rest_z.at[r, i], rz_send.at[r, i], rz_recv.at[r, i], {"zl": z_rel(i)}
            )

    def rest_total(r):
        total = terms[r, rest_of(NL - 1), :].astype(F32)
        for i in range(NL - 1):
            arrived(rest_z.at[r, i], rz_recv.at[r, i])
            total = total + rest_z[r, i].astype(F32)
        return total

    def rest_over_y(r):
        rest_sum[r] = rest_total(r).astype(BF)
        send(rest_sum.at[r], rest_y.at[r], ry_send.at[r], ry_recv.at[r], {"y": lax.rem(y + r, NY)})

    act_copy.wait()
    term(4)
    pl.semaphore_wait(barrier, len(peers) + 12 - own_half.astype(jnp.int32))

    step = (1, NY - 1)

    def chain(k):
        for i in range(NL):
            rows = rows_of(i)
            for d in range(2):
                r = (step[d] * k) % NY
                half = slice(d * 128, (d + 1) * 128)
                cols = half if k == 4 else slice(0, COLS)
                if k < 4:
                    got = half if k == 3 else slice(0, COLS)
                    arrived(ring.at[d, k, i, :, got], y_recv.at[d, k, i])
                    total = terms[r, rows, got].astype(F32) + ring[d, k, i, :, got].astype(F32)
                    terms[r, rows, got] = total.astype(BF)
                send(
                    terms.at[r, rows, cols], ring.at[d, k - 1, i, :, cols],
                    y_send.at[d, k, i], y_recv.at[d, k - 1, i], {"y": lax.rem(y + step[d], NY)},
                )

    chain(4)
    rest_over_z(4)
    for r in (3, 5):
        term(r)
        rest_over_z(r)
    chain(3)
    for r in (2, 6):
        term(r)
        rest_over_z(r)
    rest_over_y(4)
    chain(2)
    for r in (1, 7, 0):
        term(r)
        rest_over_z(r)
    for r in (3, 5):
        rest_over_y(r)
    chain(1)
    for r in (2, 6, 1, 7):
        rest_over_y(r)

    for i in range(NL):
        rows = rows_of(i)
        for d in range(2):
            arrived(ring.at[d, 0, i], y_recv.at[d, 0, i])
        total = terms[0, rows, :].astype(F32) + ring[0, 0, i].astype(F32) + ring[1, 0, i].astype(F32)
        if i < NL - 1:
            terms[0, rows, :] = total.astype(BF)
            send(terms.at[0, rows, :], ring_z.at[i], z_send.at[i], z_recv.at[i], {"zl": z_rel(i)})
    for copy in prompt_copies:
        copy.wait()
    for i in range(NL - 1):
        send(own_prompts, prompts.at[zl], p_send.at[i], p_recv.at[i], {"zl": z_rel(i)})
    prompts[zl] = own_prompts[...]
    for copy in state_copies:
        copy.wait()

    def update(at, grad):
        new_one = 0.9 * state[1, at] + 0.1 * grad
        new_two = 0.999 * state[2, at] + 0.001 * grad * grad
        first = new_one / (1.0 - 0.9**50)
        second = new_two / (1.0 - 0.999**50)
        old = state[0, at]
        new_master = old - 0.003 * (first / (jnp.sqrt(second) + 1e-08) + 0.01 * old)
        weight[0, at] = new_master.astype(BF)
        new_state[0, at] = new_master
        new_state[1, at] = new_one
        new_state[2, at] = new_two

    grad = rest_total(0)
    for r in (4, 3, 5, 2, 6, 1, 7):
        arrived(rest_y.at[r], ry_recv.at[r])
        grad = grad + rest_y[r].astype(F32)
    update(slice(FIRST_Y, ROWS), grad)
    grad = total
    for i in range(NL - 1):
        arrived(ring_z.at[i], z_recv.at[i])
        grad = grad + ring_z[i].astype(F32)
    update(slice(0, FIRST_Y), grad)

    def piece(place, n):
        return weight.at[place, pl.ds((n // 2) * 80, 80), pl.ds((n % 2) * 128, 128)]

    def held(d, s):
        return SLOT[(NY - step[d] * s) % NY]

    def pass_on(s, n, d, hops=1):
        send(
            piece(held(d, s - 1), n), piece(held(d, s - 2 + hops + 1), n), w_send.at[d, s - 2 + hops, n],
            w_recv.at[d, s - 2 + hops, n], {"y": lax.rem(y + hops * step[d], NY)},
        )

    def landed(s, n, d):
        arrived(piece(held(d, s), n), w_recv.at[d, s - 1, n])

    x_order = (2, 1, 3, 0)

    def project(g, i, core):
        x_to = lax.rem(x + x_order[i], NX)
        lhs = jnp.concatenate([prompts[2 * core + n, x_to].reshape(SUB, COLS) for n in range(2)], axis=0)
        rhs = weight[4 * g : 4 * g + 4].reshape(OUTS, COLS)
        return lax.dot_general(lhs, rhs, (((1,), (1,)), ((), ())), preferred_element_type=F32)

    def project_all(g):
        for i in range(NX):
            core_out[g, i] = project(g, i, 1 - c).astype(BF)
            send(core_out.at[g, i], core_in.at[g, i], c_send.at[g, i], c_recv.at[g, i], {"c": 1 - c})
        for i in range(NX):
            own_part[g, i] = project(g, i, c)

    x_dir = (1, NX - 1)

    def part_sum(g, i, n):
        rows = slice(n * SUB, (n + 1) * SUB)
        return own_part[g, i, rows, :] + core_in[g, i, rows, :].astype(F32)

    def x_send_to(g, d, i, n, k):
        send(
            x_out.at[g, i, n], x_in.at[g, d, k, n], x_send.at[g, d, k, n], x_recv.at[g, d, k, n],
            {"x": lax.rem(x + x_dir[d], NX)},
        )

    def far(g):
        arrived(core_in.at[g, 0], c_recv.at[g, 0])
        for d in range(2):
            x_out[g, 0, d] = part_sum(g, 0, d).astype(BF)
            x_send_to(g, d, 0, d, 1)

    def near(g, d, n):
        total = part_sum(g, 1 + d, n)
        if n == d:
            arrived(x_in.at[g, d, 1, n], x_recv.at[g, d, 1, n])
            total = total + x_in[g, d, 1, n].astype(F32)
        x_out[g, 1 + d, n] = total.astype(BF)
        x_send_to(g, d, 1 + d, n, 0)

    def x_first(g):
        far(g)
        for d in range(2):
            arrived(core_in.at[g, 1 + d], c_recv.at[g, 1 + d])
            near(g, d, 1 - d)

    def x_second(g):
        for d in range(2):
            near(g, d, d)
        arrived(core_in.at[g, 3], c_recv.at[g, 3])

    def over_z(g):
        for n in range(2):
            total = part_sum(g, 3, n)
            for d in range(2):
                arrived(x_in.at[g, d, 0, n], x_recv.at[g, d, 0, n])
                total = total + x_in[g, d, 0, n].astype(F32)
            z_out[g, n] = total.astype(BF).reshape(NH, 16, OUTS)
            for h in range(NH):
                to = h * NL + 2 * c + n
                stays = jnp.logical_and(me == to, c == g)

                @pl.when(stays)
                def _():
                    z_in[me] = z_out[g, n, h]

                @pl.when(jnp.logical_not(stays))
                def _():
                    go(
                        z_out.at[g, n, h], z_in.at[me], f_send.at[g, n, h], f_recv.at[me],
                        {"zh": h, "zl": 2 * c + n, "c": g},
                    )

    for n in range(4):
        for d in range(2):
            pass_on(1, n, d)
    state_copy = pltpu.make_async_copy(new_state, state_out, store_sem.at[0])
    state_copy.start()
    for n in range(4):
        for d in range(2):
            landed(1, n, d)
            pass_on(2, n, d)
    for n in range(4):
        for d in range(2):
            landed(2, n, d)
            if n // 2 == d:
                pass_on(3, n, d, 2)
            pass_on(3, n, d)
    for i in range(NL - 1):
        arrived(prompts.at[0], p_recv.at[i])
    project_all(0)
    x_first(0)
    for n in range(4):
        for d in range(2):
            landed(3, n, d)
            if n // 2 == d:
                landed(4, n, d)
    project_all(1)
    x_second(0)
    x_first(1)
    over_z(0)
    x_second(1)
    over_z(1)

    for at in range(NZ):

        @pl.when(jnp.logical_or(me != at, jnp.logical_not(own_half)))
        def _():
            arrived(z_in.at[at], f_recv.at[at])

    for n in range(NL):
        half_sum[n] = z_in[n].astype(F32) + z_in[NL + n].astype(F32) + z_in[2 * NL + n].astype(F32)
    theirs = pl.ds(pl.multiple_of(8 * (1 - c), 8), 8)
    mine = pl.ds(pl.multiple_of(8 * c, 8), 8)
    send(half_sum.at[:, theirs, :], half_in, h_send.at[0], h_recv.at[0], {"c": 1 - c})

    def lay_out(group, read):
        parts = [read(n) for n in range(NL)]
        for j in range(4):
            block = jnp.concatenate([part[:, j * ROWS : (j + 1) * ROWS] for part in parts], axis=1)
            far_y = lax.rem(y + PLACE[j] + group * (PLACE[4 + j] - PLACE[j]), NY)
            proj[:, pl.ds(pl.multiple_of(far_y * 640, 640), 640)] = block.astype(BF)

    lay_out(c, lambda n: half_sum[n, mine, :])
    arrived(half_in, h_recv.at[0])
    lay_out(1 - c, lambda n: half_in[n])
    last = pltpu.make_async_copy(proj, proj_out, store_sem.at[1])
    last.start()

    for copy in sent:
        copy.wait_send()
    for g in range(2):
        for n in range(2):
            for h in range(NH):

                @pl.when(jnp.logical_or(me != h * NL + 2 * c + n, c != g))
                def _():
                    pltpu.make_async_copy(z_out.at[g, n, h], z_out.at[g, n, h], f_send.at[g, n, h]).wait()

    state_copy.wait()
    last.wait()


def hand_on(state, proj, master_out, one_out, two_out, proj_out, held, held_proj, in_sem, out_sem):
    moves = [(proj, held_proj, proj_out)]
    moves += [(state.at[i], held.at[i], ref) for i, ref in enumerate((master_out, one_out, two_out))]
    reads = [pltpu.make_async_copy(src, mid, in_sem.at[i]) for i, (src, mid, _) in enumerate(moves)]
    writes = [pltpu.make_async_copy(mid, dst, out_sem.at[i]) for i, (_, mid, dst) in enumerate(moves)]
    for copy in reads:
        copy.start()
    for read, write in zip(reads, writes):
        read.wait()
        write.start()
    for copy in writes:
        copy.wait()


def local(activations, cotangent, master, moment_one, moment_two, prompts):
    any_space = pl.BlockSpec(memory_space=pl.ANY)
    dma = pltpu.SemaphoreType.DMA
    state, proj = pl.pallas_call(
        kernel,
        out_shape=(jax.ShapeDtypeStruct((3, ROWS, COLS), F32), jax.ShapeDtypeStruct((8, 5120), BF)),
        in_specs=[any_space] * 6,
        out_specs=[any_space] * 2,
        scratch_shapes=[
            pltpu.VMEM((512, COLS), BF),
            pltpu.VMEM((NY, 512, 640), BF),
            pltpu.VMEM((3, ROWS, COLS), F32),
            pltpu.VMEM((3, ROWS, COLS), F32),
            pltpu.VMEM((NX, NH, 16, COLS), BF),
            pltpu.VMEM((NL, NX, NH, 16, COLS), BF),
            pltpu.VMEM((NY, 640, COLS), BF),
            pltpu.VMEM((2, 4, NL, FIRST_Y, COLS), BF),
            pltpu.VMEM((NL - 1, FIRST_Y, COLS), BF),
            pltpu.VMEM((NY, NL - 1, REST, COLS), BF),
            pltpu.VMEM((NY, REST, COLS), BF),
            pltpu.VMEM((NY, REST, COLS), BF),
            pltpu.VMEM((NY, ROWS, COLS), BF),
            pltpu.VMEM((2, NX, 2 * SUB, OUTS), F32),
            pltpu.VMEM((2, NX, 2 * SUB, OUTS), BF),
            pltpu.VMEM((2, NX, 2 * SUB, OUTS), BF),
            pltpu.VMEM((2, 3, 2, SUB, OUTS), BF),
            pltpu.VMEM((2, 2, 2, 2, SUB, OUTS), BF),
            pltpu.VMEM((2, 2, NH, 16, OUTS), BF),
            pltpu.VMEM((NZ, 16, OUTS), BF),
            pltpu.VMEM((NL, 16, OUTS), F32),
            pltpu.VMEM((NL, 8, OUTS), F32),
            pltpu.VMEM((8, 5120), BF),
            dma((8,)), dma((NY,)), dma((2,)),
            dma((3,)), dma((3,)),
            dma((2, 5, NL)), dma((2, 4, NL)),
            dma((3,)), dma((3,)),
            dma((NY, 3)), dma((NY, 3)),
            dma((NY,)), dma((NY,)),
            dma((2, 4, 4)), dma((2, 4, 4)),
            dma((2, NX)), dma((2, NX)),
            dma((2, 2, 2, 2)), dma((2, 2, 2, 2)),
            dma((2, 2, NH)), dma((NZ,)),
            dma((1,)), dma((1,)),
        ],
        compiler_params=pltpu.CompilerParams(collective_id=0, has_side_effects=True),
        name="step",
    )(activations, cotangent, master, moment_one, moment_two, prompts.reshape(NH, NX, 16, COLS))
    weight_shape = jax.ShapeDtypeStruct((ROWS, COLS), F32)
    return pl.pallas_call(
        hand_on,
        out_shape=(weight_shape, weight_shape, weight_shape, jax.ShapeDtypeStruct((8, 5120), BF)),
        in_specs=[any_space] * 2,
        out_specs=[any_space] * 4,
        scratch_shapes=[pltpu.VMEM((3, ROWS, COLS), F32), pltpu.VMEM((8, 5120), BF), dma((4,)), dma((4,))],
        name="hand_on",
    )(state, proj)


def solution(mesh):
    torus = Mesh(mesh.devices.reshape(NY, NL, NH, NX, NC), AXES)
    dp, tensor = ("y", "zl"), ("zh", "x", "c")
    both = P(dp, tensor)
    in_specs = (both, P(dp, None), both, both, both, both)
    out_specs = (both, both, both, P(dp + tensor, None))
    return jax.shard_map(local, mesh=torus, in_specs=in_specs, out_specs=out_specs, check_vma=False)
```

time: 93.7 us -> 83.3 us (0.89)
  local copies, waits for them, and re-layouts: 6.3 us -> 0 us
  Pallas kernels: 86.5 us -> 82.5 us
    unnamed x4 -> x0, local copies, waits for them, and re-layouts: 6.3 us -> none
    pallas_call x1 -> x2, Pallas kernels: 86.5 us -> 82.5 us  [the longest x1 80.6 us: local(): pl.pallas_call(kernel, out_shape=(jax.ShapeDtypeStruct((3, ROWS, COLS), F...]
where the time goes in v2:
time: 83.3 us; the launch traced here: 83.1 us
  Pallas kernels  82.5 us (99%)
    pallas_call x1, Pallas kernels, local(): pl.pallas_call(kernel, out_shape=(jax.ShapeDtypeStruct((3, ROWS, COLS), F...  80.6 us
    pallas_call x1, Pallas kernels, local(): pl.pallas_call(hand_on, out_shape=(weight_shape, weight_shape, weight_sha...  1.85 us

profile of v2, /device:TPU:1, one launch (start us, length us, event | category | flops | bytes accessed | tf_op | source)
XLA Modules:
  0.0 83.1 jit_solution(931627325917605201)
XLA Ops:
  0.6 80.6 %step.1 = (f32[3,160,256]{2,1,0:T(8,128)}, bf16[8,5120]{1,0:T(8,128)(2,1)}) custom-call(bf16[512,256]{1,0:T(8,128)(2,1)} %act_hbm.1, bf16[512,5120]{1,0:T(8,128)(2,1)} %cot_hbm.1, f32[160,256]{1,0:T(8,128)} %master_hbm.1, f32[160,256]{1,0:T(8,128)} %one_hbm.1, f32[160,256]{1,0:T(8,128)} %two_hbm.1, bf16[3,4,16,256]{3,2,1,0:T(8,128)(2,1)} %bitcast.1), custom_call_target="tpu_custom_call" | custom-call | tf_op jit(solution)/shard_map/step/pallas_call | solution.py:380
  81.3 1.8 %hand_on.1 = (f32[160,256]{1,0:T(8,128)}, f32[160,256]{1,0:T(8,128)}, f32[160,256]{1,0:T(8,128)}, bf16[8,5120]{1,0:T(8,128)(2,1)}) custom-call(f32[3,160,256]{2,1,0:T(8,128)} %get-tuple-element.6.state, bf16[8,5120]{1,0:T(8,128)(2,1)} %get-tuple-element.7.proj), custom_call_target="tpu_custom_call" | custom-call | tf_op jit(solution)/shard_map/hand_on/pallas_call | solution.py:425

commit v3 on v2

v3 whole, which is shorter than its diff:
```python
import jax
import jax.numpy as jnp
from jax import lax
from jax.experimental import pallas as pl
from jax.experimental.pallas import tpu as pltpu
from jax.sharding import Mesh
from jax.sharding import PartitionSpec as P

AXES = ("y", "zl", "zh", "x", "c")
NY, NL, NH, NX, NC = 8, 4, 3, 4, 2
NZ = NL * NH
BF = jnp.bfloat16
F32 = jnp.float32

ROWS = 160
FIRST_Y = 112
REST = ROWS - FIRST_Y
HALF = ((0, 64), (64, 48))
COLS = 256
OUTS = 4 * ROWS
SUB = NH * 16
PLACE = (0, 1, 7, 2, 6, 3, 5, 4)
SLOT = tuple(PLACE.index(r) for r in range(NY))
PIECE = ((0, 48), (48, 32), (80, 48), (128, 32))
MESH = pl.DeviceIdType.MESH


def kernel(
    act_hbm, cot_hbm, master_hbm, one_hbm, two_hbm, prompts_hbm,
    state_out, z_in,
    act, cot, state, new_state, own_prompts, prompts, terms, ring, ring_z, rest_z, rest_y, rest_sum,
    weight, own_part, core_out, core_in, x_out, x_in, z_out,
    load_sem, cot_sem, store_sem, p_send, p_recv, y_send, y_recv, z_send, z_recv,
    rz_send, rz_recv, ry_send, ry_recv,
    w_send, w_recv, c_send, c_recv, x_send, x_recv, f_send, f_recv,
    up_edge, up_group, down_edge, down_group,
):
    y, zl, zh, x, c = (lax.axis_index(axis) for axis in AXES)
    sent = []

    def go(src, dst, send_sem, recv_sem, to):
        copy = pltpu.make_async_remote_copy(
            src_ref=src, dst_ref=dst, send_sem=send_sem, recv_sem=recv_sem,
            device_id=to, device_id_type=MESH,
        )
        copy.start()
        return copy

    def send(src, dst, send_sem, recv_sem, to):
        sent.append(go(src, dst, send_sem, recv_sem, to))

    def arrived(dst, recv_sem):
        pltpu.make_async_copy(dst, dst, recv_sem).wait()

    def cot_copy(r):
        first = pl.multiple_of(lax.rem(y + r, NY) * 640, 640)
        return pltpu.make_async_copy(cot_hbm.at[:, pl.ds(first, 640)], cot.at[r], cot_sem.at[r])

    act_copy = pltpu.make_async_copy(act_hbm, act, load_sem.at[0])
    act_copy.start()
    for r in (4, 3, 5, 2, 6, 1, 7, 0):
        cot_copy(r).start()
    prompt_copies = [
        pltpu.make_async_copy(prompts_hbm.at[:, i], own_prompts.at[i], load_sem.at[1 + i]) for i in range(NX)
    ]
    state_copies = [
        pltpu.make_async_copy(ref, state.at[i], load_sem.at[5 + i])
        for i, ref in enumerate((master_hbm, one_hbm, two_hbm))
    ]
    for copy in prompt_copies + state_copies:
        copy.start()

    barrier = pltpu.get_barrier_semaphore()
    peers = [{"y": lax.rem(y + i, NY)} for i in range(1, NY)]
    peers += [{"zl": lax.rem(zl + i, NL)} for i in range(1, NL)]
    peers += [{"x": lax.rem(x + 1, NX)}, {"x": lax.rem(x + NX - 1, NX)}, {"c": 1 - c}]
    for peer in peers:
        pl.semaphore_signal(barrier, inc=1, device_id=peer, device_id_type=MESH)
    me = zh * NL + zl
    lower_edge = jnp.logical_and(zl == 0, zh > 0)
    upper_edge = jnp.logical_and(zl == NL - 1, zh < NH - 1)

    def tell(semaphore, peer):
        pl.semaphore_signal(semaphore, inc=1, device_id=peer, device_id_type=MESH)

    pl.when(lower_edge)(lambda: tell(barrier, {"zh": zh - 1, "zl": NL - 1}))
    pl.when(upper_edge)(lambda: tell(barrier, {"zh": zh + 1, "zl": 0}))

    def at(h, n):
        return jnp.logical_and(zh == h, zl == n)

    def tell_group(semaphore):
        for i in range(1, NL):
            tell(semaphore, {"zl": lax.rem(zl + i, NL)})

    def word_1():
        pl.when(at(0, 3))(lambda: tell(up_edge, {"zh": 1, "zl": 0}))
        pl.when(at(2, 0))(lambda: tell(down_edge, {"zh": 1, "zl": 3}))

    def hear_and_tell_group(h, n, edge, group):
        @pl.when(at(h, n))
        def _():
            pl.semaphore_wait(edge, 1)
            tell_group(group)

    def word_2():
        hear_and_tell_group(1, 0, up_edge, up_group)
        hear_and_tell_group(1, 3, down_edge, down_group)

    def word_3():
        @pl.when(at(1, 3))
        def _():
            pl.semaphore_wait(up_group, 1)
            tell(up_edge, {"zh": 2, "zl": 0})

        @pl.when(at(1, 0))
        def _():
            pl.semaphore_wait(down_group, 1)
            tell(down_edge, {"zh": 0, "zl": 3})

    def word_4():
        hear_and_tell_group(2, 0, up_edge, up_group)
        hear_and_tell_group(0, 3, down_edge, down_group)

    def word_5():
        middle = jnp.logical_and(zh == 1, jnp.logical_or(zl == 1, zl == 2))
        below = jnp.logical_or(middle, jnp.logical_and(zh == 2, zl != 0))
        above = jnp.logical_or(middle, jnp.logical_and(zh == 0, zl != 3))
        pl.when(below)(lambda: pl.semaphore_wait(up_group, 1))
        pl.when(above)(lambda: pl.semaphore_wait(down_group, 1))

    def term(r):
        cot_copy(r).wait()
        for b in range(5):
            block = lax.dot_general(
                cot[r, :, b * 128 : (b + 1) * 128], act[...],
                (((0,), (0,)), ((), ())), preferred_element_type=F32,
            )
            terms[r, b * 128 : (b + 1) * 128, :] = block.astype(BF)

    def z_rel(i):
        return lax.rem(zl + 1 + i, NL)

    def rows_of(i, first=0, size=FIRST_Y):
        return pl.ds(pl.multiple_of(z_rel(i) * ROWS + first, 16), size)

    def rest_of(i):
        return pl.ds(pl.multiple_of(z_rel(i) * ROWS + FIRST_Y, 16), REST)

    def rest_over_z(r):
        for i in range(NL - 1):
            send(
                terms.at[r, rest_of(i), :], rest_z.at[r, i], rz_send.at[r, i], rz_recv.at[r, i], {"zl": z_rel(i)}
            )

    def rest_total(r):
        total = terms[r, rest_of(NL - 1), :].astype(F32)
        for i in range(NL - 1):
            arrived(rest_z.at[r, i], rz_recv.at[r, i])
            total = total + rest_z[r, i].astype(F32)
        return total

    def rest_over_y(r):
        rest_sum[r] = rest_total(r).astype(BF)
        send(rest_sum.at[r], rest_y.at[r], ry_send.at[r], ry_recv.at[r], {"y": lax.rem(y + r, NY)})

    act_copy.wait()
    term(4)
    pl.semaphore_wait(barrier, len(peers) + lower_edge.astype(jnp.int32) + upper_edge.astype(jnp.int32))

    step = (1, NY - 1)

    def chain(k):
        for i in range(NL):
            for d in range(2):
                r = (step[d] * k) % NY
                half = HALF[d]
                if k < 4:
                    first, size = half if k == 3 else (0, FIRST_Y)
                    got, to = rows_of(i, first, size), pl.ds(first, size)
                    arrived(ring.at[d, k, i, to], y_recv.at[d, k, i])
                    total = terms[r, got, :].astype(F32) + ring[d, k, i, to].astype(F32)
                    terms[r, got, :] = total.astype(BF)
                first, size = half if k == 4 else (0, FIRST_Y)
                send(
                    terms.at[r, rows_of(i, first, size), :], ring.at[d, k - 1, i, pl.ds(first, size)],
                    y_send.at[d, k, i], y_recv.at[d, k - 1, i], {"y": lax.rem(y + step[d], NY)},
                )

    chain(4)
    rest_over_z(4)
    for r in (3, 5):
        term(r)
        rest_over_z(r)
    chain(3)
    for r in (2, 6):
        term(r)
        rest_over_z(r)
    rest_over_y(4)
    word_1()
    chain(2)
    for r in (1, 7, 0):
        term(r)
        rest_over_z(r)
    for r in (3, 5):
        rest_over_y(r)
    chain(1)
    for r in (2, 6, 1, 7):
        rest_over_y(r)
    word_2()

    for i in range(NL):
        rows = rows_of(i)
        for d in range(2):
            arrived(ring.at[d, 0, i], y_recv.at[d, 0, i])
        total = terms[0, rows, :].astype(F32) + ring[0, 0, i].astype(F32) + ring[1, 0, i].astype(F32)
        if i < NL - 1:
            terms[0, rows, :] = total.astype(BF)
            send(terms.at[0, rows, :], ring_z.at[i], z_send.at[i], z_recv.at[i], {"zl": z_rel(i)})
    for copy in prompt_copies:
        copy.wait()
    for i in range(NL - 1):
        send(own_prompts, prompts.at[zl], p_send.at[i], p_recv.at[i], {"zl": z_rel(i)})
    prompts[zl] = own_prompts[...]
    word_3()
    for copy in state_copies:
        copy.wait()

    def update(at, grad):
        new_one = 0.9 * state[1, at] + 0.1 * grad
        new_two = 0.999 * state[2, at] + 0.001 * grad * grad
        first = new_one / (1.0 - 0.9**50)
        second = new_two / (1.0 - 0.999**50)
        old = state[0, at]
        new_master = old - 0.003 * (first / (jnp.sqrt(second) + 1e-08) + 0.01 * old)
        weight[0, at] = new_master.astype(BF)
        new_state[0, at] = new_master
        new_state[1, at] = new_one
        new_state[2, at] = new_two

    grad = rest_total(0)
    for r in (4, 3, 5, 2, 6, 1, 7):
        arrived(rest_y.at[r], ry_recv.at[r])
        grad = grad + rest_y[r].astype(F32)
    update(slice(FIRST_Y, ROWS), grad)
    grad = total
    for i in range(NL - 1):
        arrived(ring_z.at[i], z_recv.at[i])
        grad = grad + ring_z[i].astype(F32)
    update(slice(0, FIRST_Y), grad)

    def piece(place, n):
        return weight.at[place, pl.ds(*PIECE[n])]

    def held(d, s):
        return SLOT[(NY - step[d] * s) % NY]

    def pass_on(s, n, d, hops=1):
        send(
            piece(held(d, s - 1), n), piece(held(d, s - 2 + hops + 1), n), w_send.at[d, s - 2 + hops, n],
            w_recv.at[d, s - 2 + hops, n], {"y": lax.rem(y + hops * step[d], NY)},
        )

    def landed(s, n, d):
        arrived(piece(held(d, s), n), w_recv.at[d, s - 1, n])

    x_order = (2, 1, 3, 0)

    def project(g, core):
        lhs = [prompts[2 * core + n, lax.rem(x + far_x, NX)].reshape(SUB, COLS) for far_x in x_order for n in range(2)]
        rhs = weight[4 * g : 4 * g + 4].reshape(OUTS, COLS)
        return lax.dot_general(
            jnp.concatenate(lhs, axis=0), rhs, (((1,), (1,)), ((), ())), preferred_element_type=F32
        )

    def project_all(g):
        theirs = project(g, 1 - c)
        for i in range(NX):
            core_out[g, i] = theirs[i * 2 * SUB : (i + 1) * 2 * SUB].astype(BF)
            send(core_out.at[g, i], core_in.at[g, i], c_send.at[g, i], c_recv.at[g, i], {"c": 1 - c})
        own_part[g] = project(g, c).reshape(NX, 2 * SUB, OUTS)

    x_dir = (1, NX - 1)

    def part_sum(g, i, n, h):
        rows = slice(n * SUB + h * 16, n * SUB + (h + 1) * 16)
        return own_part[g, i, rows, :] + core_in[g, i, rows, :].astype(F32)

    def x_send_to(g, d, i, n, k, h):
        send(
            x_out.at[g, i, n, h], x_in.at[g, d, k, n, h], x_send.at[g, d, k, n, h], x_recv.at[g, d, k, n, h],
            {"x": lax.rem(x + x_dir[d], NX)},
        )

    def far(g, d, h):
        x_out[g, 0, d, h] = part_sum(g, 0, d, h).astype(BF)
        x_send_to(g, d, 0, d, 1, h)

    def near(g, d, n, h):
        total = part_sum(g, 1 + d, n, h)
        if n == d:
            arrived(x_in.at[g, d, 1, n, h], x_recv.at[g, d, 1, n, h])
            total = total + x_in[g, d, 1, n, h].astype(F32)
        x_out[g, 1 + d, n, h] = total.astype(BF)
        x_send_to(g, d, 1 + d, n, 0, h)

    def x_first(g):
        arrived(core_in.at[g, 0], c_recv.at[g, 0])
        for h in range(NH):
            for d in range(2):
                far(g, d, h)
        for d in range(2):
            arrived(core_in.at[g, 1 + d], c_recv.at[g, 1 + d])
        for h in range(NH):
            for d in range(2):
                near(g, d, 1 - d, h)

    def x_second(g):
        for h in range(NH):
            for d in range(2):
                near(g, d, d, h)
        arrived(core_in.at[g, 3], c_recv.at[g, 3])

    def over_z(g):
        for h in range(NH):
            for n in range(2):
                total = part_sum(g, 3, n, h)
                for d in range(2):
                    arrived(x_in.at[g, d, 0, n, h], x_recv.at[g, d, 0, n, h])
                    total = total + x_in[g, d, 0, n, h].astype(F32)
                z_out[g, n, h] = total.reshape(NC, 8, OUTS).astype(BF)
                for core in range(NC):
                    stays = jnp.logical_and(me == h * NL + 2 * c + n, c == core)

                    @pl.when(stays)
                    def _():
                        pltpu.make_async_copy(z_out.at[g, n, h, core], z_in.at[g, me], f_recv.at[g, me]).start()

                    @pl.when(jnp.logical_not(stays))
                    def _():
                        go(
                            z_out.at[g, n, h, core], z_in.at[g, me], f_send.at[g, n, h, core], f_recv.at[g, me],
                            {"zh": h, "zl": 2 * c + n, "c": core},
                        )

    for n in range(4):
        for d in range(2):
            pass_on(1, n, d)
    state_copy = pltpu.make_async_copy(new_state, state_out, store_sem)
    state_copy.start()
    for n in range(4):
        for d in range(2):
            landed(1, n, d)
            pass_on(2, n, d)
    for n in range(4):
        for d in range(2):
            landed(2, n, d)
            if n // 2 == d:
                pass_on(3, n, d, 2)
            pass_on(3, n, d)
    word_4()
    for i in range(NL - 1):
        arrived(prompts.at[0], p_recv.at[i])
    project_all(0)
    x_first(0)
    for n in range(4):
        for d in range(2):
            landed(3, n, d)
            if n // 2 == d:
                landed(4, n, d)
    word_5()
    project_all(1)
    x_second(0)
    x_first(1)
    over_z(0)
    x_second(1)
    over_z(1)

    for copy in sent:
        copy.wait_send()
    for g in range(2):
        for n in range(2):
            for h in range(NH):
                for core in range(NC):

                    @pl.when(jnp.logical_or(me != h * NL + 2 * c + n, c != core))
                    def _():
                        part = z_out.at[g, n, h, core]
                        pltpu.make_async_copy(part, part, f_send.at[g, n, h, core]).wait()

        for source in range(NZ):
            arrived(z_in.at[g, source], f_recv.at[g, source])
    state_copy.wait()


def finish(
    state, z_in, master_out, one_out, two_out, proj_out, held, parts, proj, read_sem, in_sem, out_sem
):
    y = lax.axis_index("y")
    read = pltpu.make_async_copy(z_in, parts, read_sem)
    read.start()
    outs = (master_out, one_out, two_out)
    reads = [pltpu.make_async_copy(state.at[i], held.at[i], in_sem.at[i]) for i in range(3)]
    writes = [pltpu.make_async_copy(held.at[i], outs[i], out_sem.at[i]) for i in range(3)]
    for copy in reads:
        copy.start()
    read.wait()
    for g in range(2):
        sums = []
        for n in range(NL):
            terms = [parts[g, h * NL + n].astype(F32) for h in range(NH)]
            sums.append(terms[0] + terms[1] + terms[2])
        for j in range(4):
            block = jnp.concatenate([part[:, j * ROWS : (j + 1) * ROWS] for part in sums], axis=1)
            far_y = lax.rem(y + PLACE[4 * g + j], NY)
            proj[:, pl.ds(pl.multiple_of(far_y * 640, 640), 640)] = block.astype(BF)
    last = pltpu.make_async_copy(proj, proj_out, out_sem.at[3])
    last.start()
    for copy, write in zip(reads, writes):
        copy.wait()
        write.start()
    for copy in writes:
        copy.wait()
    last.wait()


def local(activations, cotangent, master, moment_one, moment_two, prompts):
    any_space = pl.BlockSpec(memory_space=pl.ANY)
    dma = pltpu.SemaphoreType.DMA
    state, z_in = pl.pallas_call(
        kernel,
        out_shape=(jax.ShapeDtypeStruct((3, ROWS, COLS), F32), jax.ShapeDtypeStruct((2, NZ, 8, OUTS), BF)),
        in_specs=[any_space] * 6,
        out_specs=[any_space] * 2,
        scratch_shapes=[
            pltpu.VMEM((512, COLS), BF),
            pltpu.VMEM((NY, 512, 640), BF),
            pltpu.VMEM((3, ROWS, COLS), F32),
            pltpu.VMEM((3, ROWS, COLS), F32),
            pltpu.VMEM((NX, NH, 16, COLS), BF),
            pltpu.VMEM((NL, NX, NH, 16, COLS), BF),
            pltpu.VMEM((NY, 640, COLS), BF),
            pltpu.VMEM((2, 4, NL, FIRST_Y, COLS), BF),
            pltpu.VMEM((NL - 1, FIRST_Y, COLS), BF),
            pltpu.VMEM((NY, NL - 1, REST, COLS), BF),
            pltpu.VMEM((NY, REST, COLS), BF),
            pltpu.VMEM((NY, REST, COLS), BF),
            pltpu.VMEM((NY, ROWS, COLS), BF),
            pltpu.VMEM((2, NX, 2 * SUB, OUTS), F32),
            pltpu.VMEM((2, NX, 2 * SUB, OUTS), BF),
            pltpu.VMEM((2, NX, 2 * SUB, OUTS), BF),
            pltpu.VMEM((2, 3, 2, NH, 16, OUTS), BF),
            pltpu.VMEM((2, 2, 2, 2, NH, 16, OUTS), BF),
            pltpu.VMEM((2, 2, NH, NC, 8, OUTS), BF),
            dma((8,)), dma((NY,)), dma(()),
            dma((3,)), dma((3,)),
            dma((2, 5, NL)), dma((2, 4, NL)),
            dma((3,)), dma((3,)),
            dma((NY, 3)), dma((NY, 3)),
            dma((NY,)), dma((NY,)),
            dma((2, 4, 4)), dma((2, 4, 4)),
            dma((2, NX)), dma((2, NX)),
            dma((2, 2, 2, 2, NH)), dma((2, 2, 2, 2, NH)),
            dma((2, 2, NH, NC)), dma((2, NZ)),
            *[pltpu.SemaphoreType.REGULAR] * 4,
        ],
        compiler_params=pltpu.CompilerParams(collective_id=0, has_side_effects=True),
        name="step",
    )(activations, cotangent, master, moment_one, moment_two, prompts.reshape(NH, NX, 16, COLS))
    weight_shape = jax.ShapeDtypeStruct((ROWS, COLS), F32)
    return pl.pallas_call(
        finish,
        out_shape=(weight_shape, weight_shape, weight_shape, jax.ShapeDtypeStruct((8, 5120), BF)),
        in_specs=[any_space] * 2,
        out_specs=[any_space] * 4,
        scratch_shapes=[
            pltpu.VMEM((3, ROWS, COLS), F32), pltpu.VMEM((2, NZ, 8, OUTS), BF), pltpu.VMEM((8, 5120), BF),
            dma(()), dma((3,)), dma((4,)),
        ],
        name="finish",
    )(state, z_in)


def solution(mesh):
    torus = Mesh(mesh.devices.reshape(NY, NL, NH, NX, NC), AXES)
    dp, tensor = ("y", "zl"), ("zh", "x", "c")
    both = P(dp, tensor)
    in_specs = (both, P(dp, None), both, both, both, both)
    out_specs = (both, both, both, P(dp + tensor, None))
    return jax.shard_map(local, mesh=torus, in_specs=in_specs, out_specs=out_specs, check_vma=False)
```

time: 83.3 us -> 81.1 us (0.974)
  Pallas kernels: 82.5 us -> 80.3 us
    pallas_call x1, Pallas kernels: 80.6 us -> 78.3 us  [local(): pl.pallas_call(kernel, out_shape=(jax.ShapeDtypeStruct((3, ROWS, COLS), F...]
where the time goes in v3:
time: 81.1 us; the launch traced here: 81 us
  Pallas kernels  80.3 us (99%)
    pallas_call x1, Pallas kernels, local(): pl.pallas_call(kernel, out_shape=(jax.ShapeDtypeStruct((3, ROWS, COLS), F...  78.3 us
    pallas_call x1, Pallas kernels, local(): pl.pallas_call(finish, out_shape=(weight_shape, weight_shape, weight_shap...  2.07 us

profile of v3, /device:TPU:1, one launch (start us, length us, event | category | flops | bytes accessed | tf_op | source)
XLA Modules:
  0.0 81.0 jit_solution(7207804309058986759)
XLA Ops:
  0.6 78.3 %step.1 = (f32[3,160,256]{2,1,0:T(8,128)}, bf16[2,12,8,640]{3,2,1,0:T(8,128)(2,1)}) custom-call(bf16[512,256]{1,0:T(8,128)(2,1)} %act_hbm.1, bf16[512,5120]{1,0:T(8,128)(2,1)} %cot_hbm.1, f32[160,256]{1,0:T(8,128)} %master_hbm.1, f32[160,256]{1,0:T(8,128)} %one_hbm.1, f32[160,256]{1,0:T(8,128)} %two_hbm.1, bf16[3,4,16,256]{3,2,1,0:T(8,128)(2,1)} %bitcast.1), custom_call_target="tpu_custom_call" | custom-call | tf_op jit(solution)/shard_map/step/pallas_call | solution.py:430
  78.9 2.1 %finish.1 = (f32[160,256]{1,0:T(8,128)}, f32[160,256]{1,0:T(8,128)}, f32[160,256]{1,0:T(8,128)}, bf16[8,5120]{1,0:T(8,128)(2,1)}) custom-call(f32[3,160,256]{2,1,0:T(8,128)} %get-tuple-element.6.state, bf16[2,12,8,640]{3,2,1,0:T(8,128)(2,1)} %get-tuple-element.7.z_in), custom_call_target="tpu_custom_call" | custom-call | tf_op jit(solution)/shard_map/finish/pallas_call | solution.py:471

commit v4 on v3

--- a/solution.py
+++ b/solution.py
@@ -139,7 +139,14 @@
             terms[r, b * 128 : (b + 1) * 128, :] = block.astype(BF)
 
     def z_rel(i):
-        return lax.rem(zl + 1 + i, NL)
+        if i == NL - 1:
+            return zl
+        down = NL - 1 - i - (NL - 1 - i <= zl).astype(jnp.int32)
+        up = i + (i >= zl).astype(jnp.int32)
+        return down + zl // 2 * (up - down)
+
+    def slot(i):
+        return lax.rem(zl - z_rel(i) + NL, NL) - 1
 
     def rows_of(i, first=0, size=FIRST_Y):
         return pl.ds(pl.multiple_of(z_rel(i) * ROWS + first, 16), size)
@@ -150,7 +157,8 @@
     def rest_over_z(r):
         for i in range(NL - 1):
             send(
-                terms.at[r, rest_of(i), :], rest_z.at[r, i], rz_send.at[r, i], rz_recv.at[r, i], {"zl": z_rel(i)}
+                terms.at[r, rest_of(i), :], rest_z.at[r, slot(i)], rz_send.at[r, i], rz_recv.at[r, slot(i)],
+                {"zl": z_rel(i)},
             )
 
     def rest_total(r):
@@ -216,11 +224,11 @@
         total = terms[0, rows, :].astype(F32) + ring[0, 0, i].astype(F32) + ring[1, 0, i].astype(F32)
         if i < NL - 1:
             terms[0, rows, :] = total.astype(BF)
-            send(terms.at[0, rows, :], ring_z.at[i], z_send.at[i], z_recv.at[i], {"zl": z_rel(i)})
+            send(terms.at[0, rows, :], ring_z.at[slot(i)], z_send.at[i], z_recv.at[slot(i)], {"zl": z_rel(i)})
     for copy in prompt_copies:
         copy.wait()
     for i in range(NL - 1):
-        send(own_prompts, prompts.at[zl], p_send.at[i], p_recv.at[i], {"zl": z_rel(i)})
+        send(own_prompts, prompts.at[zl], p_send.at[i], p_recv.at[slot(i)], {"zl": z_rel(i)})
     prompts[zl] = own_prompts[...]
     word_3()
     for copy in state_copies:

time: 81.1 us -> 80.1 us (0.988)
  Pallas kernels: 80.3 us -> 79.3 us
    pallas_call x1, Pallas kernels: 78.3 us -> 77.2 us  [local(): pl.pallas_call(kernel, out_shape=(jax.ShapeDtypeStruct((3, ROWS, COLS), F...]
where the time goes in v4:
time: 80.1 us; the launch traced here: 80 us
  Pallas kernels  79.3 us (99%)
    pallas_call x1, Pallas kernels, local(): pl.pallas_call(kernel, out_shape=(jax.ShapeDtypeStruct((3, ROWS, COLS), F...  77.2 us
    pallas_call x1, Pallas kernels, local(): pl.pallas_call(finish, out_shape=(weight_shape, weight_shape, weight_shap...  2.07 us

profile of v4, /device:TPU:1, one launch (start us, length us, event | category | flops | bytes accessed | tf_op | source)
XLA Modules:
  0.0 80.0 jit_solution(5368785126875477429)
XLA Ops:
  0.6 77.2 %step.1 = (f32[3,160,256]{2,1,0:T(8,128)}, bf16[2,12,8,640]{3,2,1,0:T(8,128)(2,1)}) custom-call(bf16[512,256]{1,0:T(8,128)(2,1)} %act_hbm.1, bf16[512,5120]{1,0:T(8,128)(2,1)} %cot_hbm.1, f32[160,256]{1,0:T(8,128)} %master_hbm.1, f32[160,256]{1,0:T(8,128)} %one_hbm.1, f32[160,256]{1,0:T(8,128)} %two_hbm.1, bf16[3,4,16,256]{3,2,1,0:T(8,128)(2,1)} %bitcast.1), custom_call_target="tpu_custom_call" | custom-call | tf_op jit(solution)/shard_map/step/pallas_call | solution.py:438
  77.9 2.1 %finish.1 = (f32[160,256]{1,0:T(8,128)}, f32[160,256]{1,0:T(8,128)}, f32[160,256]{1,0:T(8,128)}, bf16[8,5120]{1,0:T(8,128)(2,1)}) custom-call(f32[3,160,256]{2,1,0:T(8,128)} %get-tuple-element.6.state, bf16[2,12,8,640]{3,2,1,0:T(8,128)(2,1)} %get-tuple-element.7.z_in), custom_call_target="tpu_custom_call" | custom-call | tf_op jit(solution)/shard_map/finish/pallas_call | solution.py:479
